TPU v7x, 32 devices: a whole 2x2x4 slice. The times are simulated.
32 devices in a mesh: expert: 8 (over z, x), shard: 4 (over y, core).
Axes of the slice: x: 2, y: 2, z: 4, core: 2. Of those that a mesh axis runs over, the one named last changes fastest.
Arguments:
- train_down: float32 [16, 6400, 4096], P('expert', None, 'shard'), may hold values from -0.109375 to 0.109375
- router_weight: float32 [4096, 16], P('shard', 'expert'), may hold values from -0.09375 to 0.09375
- router_gain: float32 [4096], P('shard'), may hold values from 0.25 to 1.75
Outputs:
- ready_down: bfloat16 [16, 6400, 4096], P('expert', 'shard')
- scale_down: float32 [16, 6400], P('expert', 'shard')
- serve_router: bfloat16 [4096, 16], replicated
All inputs are finite; a program needn't handle non-finite values. Where the computation divides by a largest or mean magnitude, that divisor is 1e-20 or more.
Results may differ from a plain program's by a relative error of at most 0.001.
Values may be sent and summed in bfloat16 or wider, within the bound.
A program may use at most 192 MiB of HBM per device.

v0:
```python
import jax
import jax.numpy as jnp
from jax import lax
from jax.sharding import PartitionSpec as P


def per_device(train_down, router_weight, router_gain):
    scale_down = lax.pmax(jnp.max(jnp.abs(train_down), axis=2), "shard")
    narrow_down = (train_down / jnp.expand_dims(scale_down, 2)).astype(jnp.bfloat16)
    ready_down = lax.all_to_all(narrow_down, "shard", split_axis=1, concat_axis=2, tiled=True)
    scale_down = lax.dynamic_slice_in_dim(
        scale_down, lax.axis_index("shard") * ready_down.shape[1], ready_down.shape[1], axis=1
    )
    part_router = (router_weight * router_gain[:, None]).astype(jnp.bfloat16)
    row_router = lax.all_gather(part_router, "shard", axis=0, tiled=True)
    serve_router = lax.all_gather(row_router, "expert", axis=1, tiled=True)
    return (ready_down, scale_down, serve_router)


def solution(mesh):
    in_specs = (P("expert", None, "shard"), P("shard", "expert"), P("shard"))
    out_specs = (P("expert", "shard", None), P("expert", "shard"), P())
    return jax.shard_map(
        per_device, mesh=mesh, in_specs=in_specs, out_specs=out_specs, check_vma=False
    )
```

profile of v0, /device:TPU:0, one launch (start us, length us, event | category | flops | bytes accessed | tf_op | source)
XLA Modules:
  0.0 506.3 jit_solution(6970151837764628725)
XLA Ops:
  0.6 17.0 %abs_reduce_fusion = f32[2,6400]{1,0:T(2,128)S(1)} fusion(f32[2,6400,1024]{2,1,0:T(8,128)} %param.3), kind=kLoop, calls=%fused_computation.1 | loop fusion | flops 26201600 | bytes 52480000 | tf_op jit(solution)/shard_map/reduce_max | solution.py:8
  17.6 13.4 %pmax.7 = f32[2,6400]{1,0:T(2,128)S(1)} all-reduce(f32[2,6400]{1,0:T(2,128)S(1)} %abs_reduce_fusion), channel_id=1, replica_groups=mesh['expert'=8,'shard'=4] {'shard'}, use_global_device_ids=true, to_apply=%region_1.0 | all-reduce | flops 12800 | bytes 102400 | tf_op jit(solution)/shard_map/pmax | solution.py:8
  31.1 26.1 %divide_convert_fusion = bf16[2,6400,1024]{2,1,0:T(8,128)(2,1)} fusion(f32[2,6400,1024]{2,1,0:T(8,128)} %param.3, f32[2,6400]{1,0:T(2,128)S(1)} %pmax.7), kind=kLoop, calls=%fused_computation | loop fusion | flops 26214400 | bytes 78694400 | tf_op jit(solution)/shard_map/convert_element_type | solution.py:9
  57.2 0.0 copy-start
  57.2 0.0 copy-start.1
  57.2 47.4 %copy.10 = bf16[2,6400,1024]{2,0,1:T(2,128)(2,1)} copy(bf16[2,6400,1024]{2,1,0:T(8,128)(2,1)} %divide_convert_fusion) | data formatting | bytes 52428800 | tf_op jit(solution)/shard_map/convert_element_type | solution.py:9
  104.6 8.6 %all-to-all-start = ((bf16[2,6400,1024]{2,0,1:T(2,128)(2,1)}), bf16[2,6400,1024]{2,0,1:T(2,128)(2,1)}, u32[]{:S(2)}, u32[]{:S(2)}) async-start(bf16[2,6400,1024]{2,0,1:T(2,128)(2,1)} %copy.10), calls=%async_computation | async-start | bytes 52428800 | tf_op jit(solution)/shard_map/all_to_all | solution.py:10
  113.2 0.0 copy-done
  113.2 0.0 copy-done.1
  113.2 285.0 %all_gather.6 = bf16[4096,2]{0,1:T(2,128)(2,1)S(1)} all-gather(bf16[1024,2]{0,1:T(2,128)(2,1)S(1)} %multiply_convert_fusion), channel_id=1, replica_groups=mesh['expert'=8,'shard'=4] {'shard'}, dimensions={0}, use_global_device_ids=true | all-gather | bytes 20480 | tf_op jit(solution)/shard_map/all_gather | solution.py:15
  398.2 30.8 %all-gather = bf16[8,2,4096]{2,1,0:T(2,128)(2,1)S(1)} all-gather(bf16[1,2,4096]{2,1,0:T(2,128)(2,1)S(1)} %bitcast.8), channel_id=1, replica_groups=mesh['expert'=8,'shard'=4] {'expert'}, dimensions={0}, use_global_device_ids=true | all-gather | bytes 147456 | tf_op jit(solution)/shard_map/all_gather | solution.py:16
  429.1 0.7 reshape.9
  429.8 0.7 constant_dynamic-slice_fusion
  430.5 0.0 all-to-all-done
  430.5 33.4 %copy.11 = bf16[2,1600,4,1024]{3,2,1,0:T(4,128)(2,1)} copy(bf16[2,1600,4,1024]{3,0,1,2:T(2,128)(2,1)} %bitcast.1) | data formatting | bytes 52428800 | tf_op jit(solution)/shard_map/all_to_all | solution.py:10
  463.8 42.5 %all_to_all.16 = bf16[2,1600,4096]{2,1,0:T(8,128)(2,1)} reshape(bf16[2,1600,4,1024]{3,2,1,0:T(4,128)(2,1)} %copy.11) | data formatting | bytes 52428800 | tf_op jit(solution)/shard_map/all_to_all | solution.py:10
  (1 shorter events, 0.0 us)
Async XLA Ops:
  57.2 56.0 %copy-start = (f32[1024,2]{0,1:T(2,128)S(1)}, f32[1024,2]{0,1:T(2,128)}, u32[]{:S(2)}) copy-start(f32[1024,2]{0,1:T(2,128)} %param.4) | copy-start | bytes 24580
  57.2 56.0 %copy-start.1 = (f32[1024]{0:T(1024)S(1)}, f32[1024]{0:T(1024)}, u32[]{:S(2)}) copy-start(f32[1024]{0:T(1024)} %param.5) | copy-start | bytes 12292
  104.6 325.9 %all-to-all-start = ((bf16[2,6400,1024]{2,0,1:T(2,128)(2,1)}), bf16[2,6400,1024]{2,0,1:T(2,128)(2,1)}, u32[]{:S(2)}, u32[]{:S(2)}) async-start(bf16[2,6400,1024]{2,0,1:T(2,128)(2,1)} %copy.10), calls=%async_computation | async-start | bytes 52428800 | tf_op jit(solution)/shard_map/all_to_all | solution.py:10
where the time goes:
time: 508 us; the launch traced here: 506 us
  blocking collectives  329 us (65%)
  local copies, waits for them, and re-layouts  125 us (25%)
  other arithmetic  43.2 us (9%)
  starting transfers between devices  8.59 us (2%)
    all_gather x1, blocking collectives, per_device(): row_router = lax.all_gather(part_router, 'shard', axis=0, tiled=True)  285 us
    all_to_all x2, local copies, waits for them, and re-layouts, per_device(): lax.all_to_all(narrow_down, 'shard', split_axis=1, concat_axis=2, tiled=T...  75.8 us
    convert_element_type x1, local copies, waits for them, and re-layouts, per_device(): (train_down / jnp.expand_dims(scale_down, 2)).astype(jnp.bfloat16)  47.4 us
    all_gather x1, blocking collectives, per_device(): serve_router = lax.all_gather(row_router, 'expert', axis=1, tiled=True)  30.8 us
    convert_element_type x1, other arithmetic, per_device(): (train_down / jnp.expand_dims(scale_down, 2)).astype(jnp.bfloat16)  26.1 us
    reduce_max x1, other arithmetic, per_device(): scale_down = lax.pmax(jnp.max(jnp.abs(train_down), axis=2), 'shard')  17 us
    pmax x1, blocking collectives, per_device(): scale_down = lax.pmax(jnp.max(jnp.abs(train_down), axis=2), 'shard')  13.4 us
  transfers between devices with their start and end apart: 1, of which 0 were waited for; matrix products, arithmetic and copies ran while one was open for 0% of the time, Pallas kernels for 0%

commit v1 on v0

--- a/solution.py
+++ b/solution.py
@@ -4,10 +4,17 @@
 from jax.sharding import PartitionSpec as P
 
 
+def test_group(field_in, net_axis="shard"):
+    return jnp.concatenate(
+        lax.all_to_all(jnp.stack(jnp.split(field_in, lax.axis_size(net_axis), 1)), net_axis, 0, 0),
+        2,
+    )
+
+
 def per_device(train_down, router_weight, router_gain):
     scale_down = lax.pmax(jnp.max(jnp.abs(train_down), axis=2), "shard")
     narrow_down = (train_down / jnp.expand_dims(scale_down, 2)).astype(jnp.bfloat16)
-    ready_down = lax.all_to_all(narrow_down, "shard", split_axis=1, concat_axis=2, tiled=True)
+    ready_down = test_group(narrow_down)
     scale_down = lax.dynamic_slice_in_dim(
         scale_down, lax.axis_index("shard") * ready_down.shape[1], ready_down.shape[1], axis=1
     )

time: 508 us -> 425 us (0.84)
  local copies, waits for them, and re-layouts: 125 us -> 32.6 us
  other arithmetic: 43.2 us -> 53.7 us
    all_to_all x2 -> x0, local copies, waits for them, and re-layouts: 75.8 us -> none  [per_device(): lax.all_to_all(narrow_down, 'shard', split_axis=1, concat_axis=2, tiled=T...]
    convert_element_type x1 -> x0, local copies, waits for them, and re-layouts: 47.4 us -> none  [per_device(): (train_down / jnp.expand_dims(scale_down, 2)).astype(jnp.bfloat16)]
    reshape x0 -> x1, local copies, waits for them, and re-layouts: none -> 21.7 us  [test_group(): jnp.concatenate(lax.all_to_all(jnp.stack(jnp.split(field_in, lax.axis_siz...]
    another operation x0 -> x1, other arithmetic: none -> 10.5 us  [test_group(): jnp.stack(jnp.split(field_in, lax.axis_size(net_axis), 1))]
    another operation x0 -> x1, local copies, waits for them, and re-layouts: none -> 9.52 us  [test_group(): jnp.stack(jnp.split(field_in, lax.axis_size(net_axis), 1))]
where the time goes in v1:
time: 425 us
  blocking collectives  329 us (77%)
  other arithmetic  53.7 us (13%)
  local copies, waits for them, and re-layouts  32.6 us (8%)
  starting transfers between devices  8.72 us (2%)
    all_gather x1, blocking collectives, per_device(): row_router = lax.all_gather(part_router, 'shard', axis=0, tiled=True)  285 us
    all_gather x1, blocking collectives, per_device(): serve_router = lax.all_gather(row_router, 'expert', axis=1, tiled=True)  30.8 us
    convert_element_type x1, other arithmetic, per_device(): (train_down / jnp.expand_dims(scale_down, 2)).astype(jnp.bfloat16)  26.1 us
    reshape x1, local copies, waits for them, and re-layouts, test_group(): jnp.concatenate(lax.all_to_all(jnp.stack(jnp.split(field_in, lax.axis_siz...  21.7 us
    reduce_max x1, other arithmetic, per_device(): scale_down = lax.pmax(jnp.max(jnp.abs(train_down), axis=2), 'shard')  17 us
    pmax x1, blocking collectives, per_device(): scale_down = lax.pmax(jnp.max(jnp.abs(train_down), axis=2), 'shard')  13.4 us
    another operation x1, other arithmetic, test_group(): jnp.stack(jnp.split(field_in, lax.axis_size(net_axis), 1))  10.5 us
    another operation x1, local copies, waits for them, and re-layouts, test_group(): jnp.stack(jnp.split(field_in, lax.axis_size(net_axis), 1))  9.52 us
  transfers between devices with their start and end apart: 1, of which 0 were waited for; matrix products, arithmetic and copies ran while one was open for 0% of the time, Pallas kernels for 0%

profile of v1, /device:TPU:0, one launch (start us, length us, event | category | flops | bytes accessed | tf_op | source)
XLA Modules:
  0.0 425.0 jit_solution(13586044077871705649)
XLA Ops:
  0.6 17.0 %abs_reduce_fusion = f32[2,6400]{1,0:T(2,128)S(1)} fusion(f32[2,6400,1024]{2,1,0:T(8,128)} %param.3), kind=kLoop, calls=%fused_computation.1 | loop fusion | flops 26201600 | bytes 52480000 | tf_op jit(solution)/shard_map/reduce_max | solution.py:15
  17.6 13.4 %pmax.7 = f32[2,6400]{1,0:T(2,128)S(1)} all-reduce(f32[2,6400]{1,0:T(2,128)S(1)} %abs_reduce_fusion), channel_id=1, replica_groups=mesh['expert'=8,'shard'=4] {'shard'}, use_global_device_ids=true, to_apply=%region_1.0 | all-reduce | flops 12800 | bytes 102400 | tf_op jit(solution)/shard_map/pmax | solution.py:15
  31.1 26.1 %divide_convert_fusion = bf16[2,6400,1024]{2,1,0:T(8,128)(2,1)} fusion(f32[2,6400,1024]{2,1,0:T(8,128)} %param.3, f32[2,6400]{1,0:T(2,128)S(1)} %pmax.7), kind=kLoop, calls=%fused_computation | loop fusion | flops 26214400 | bytes 78694400 | tf_op jit(solution)/shard_map/convert_element_type | solution.py:16
  57.2 9.5 %slice_bitcast_fusion.3 = (bf16[1,2,1600,1024]{3,2,1,0:T(8,128)(2,1)S(1)}, bf16[1,2,1600,1024]{3,2,1,0:T(8,128)(2,1)S(1)}, bf16[1,2,1600,1024]{3,2,1,0:T(8,128)(2,1)S(1)}, bf16[1,2,1600,1024]{3,2,1,0:T(8,128)(2,1)S(1)}) fusion(bf16[2,6400,1024]{2,1,0:T(8,128)(2,1)} %divide_convert_fusion), kind=kLoop, calls=%fused_computation.6 | loop fusion | bytes 52428800 | tf_op jit(solution)/shard_map/stack | solution.py:9
  66.7 10.5 %pad_maximum_fusion = bf16[4,2,1600,1024]{3,2,1,0:T(8,128)(2,1)} fusion(bf16[1,2,1600,1024]{3,2,1,0:T(8,128)(2,1)S(1)} %get-tuple-element.4, bf16[1,2,1600,1024]{3,2,1,0:T(8,128)(2,1)S(1)} %get-tuple-element.5, bf16[1,2,1600,1024]{3,2,1,0:T(8,128)(2,1)S(1)} %get-tuple-element.6, bf16[1,2,1600,1024]{3,2,1,0:T(8,128)(2,1)S(1)} %get-tuple-element.3), kind=kLoop, calls=%fused_computation.2 | loop fusion | flops 39321600 | bytes 52428800 | tf_op jit(solution)/shard_map/stack | solution.py:9
  77.3 0.0 copy-start
  77.3 0.0 copy-start.1
  77.3 8.7 %all-to-all-start = ((bf16[4,2,1600,1024]{3,2,1,0:T(8,128)(2,1)}), bf16[4,2,1600,1024]{3,2,1,0:T(8,128)(2,1)}, u32[]{:S(2)}, u32[]{:S(2)}) async-start(bf16[4,2,1600,1024]{3,2,1,0:T(8,128)(2,1)} %pad_maximum_fusion), calls=%async_computation | async-start | bytes 52428800 | tf_op jit(solution)/shard_map/all_to_all | solution.py:9
  86.0 0.0 copy-done
  86.0 0.0 copy-done.1
  86.0 285.0 %all_gather.6 = bf16[4096,2]{0,1:T(2,128)(2,1)S(1)} all-gather(bf16[1024,2]{0,1:T(2,128)(2,1)S(1)} %multiply_convert_fusion), channel_id=1, replica_groups=mesh['expert'=8,'shard'=4] {'shard'}, dimensions={0}, use_global_device_ids=true | all-gather | bytes 20480 | tf_op jit(solution)/shard_map/all_gather | solution.py:22
  371.0 30.8 %all-gather = bf16[8,2,4096]{2,1,0:T(2,128)(2,1)S(1)} all-gather(bf16[1,2,4096]{2,1,0:T(2,128)(2,1)S(1)} %bitcast.17), channel_id=1, replica_groups=mesh['expert'=8,'shard'=4] {'expert'}, dimensions={0}, use_global_device_ids=true | all-gather | bytes 147456 | tf_op jit(solution)/shard_map/all_gather | solution.py:23
  401.9 0.7 reshape.17
  402.6 0.7 constant_dynamic-slice_fusion
  403.3 0.0 all-to-all-done
  403.3 21.7 %copy.8 = bf16[4,2,200,8,1024]{4,3,0,2,1:T(8,128)(2,1)} copy(bf16[4,2,200,8,1024]{4,3,2,1,0:T(8,128)(2,1)} %bitcast.9) | data formatting | bytes 52428800 | tf_op jit(solution)/shard_map/reshape | solution.py:8
  (1 shorter events, 0.0 us)
Async XLA Ops:
  77.3 8.7 %copy-start = (f32[1024,2]{0,1:T(2,128)S(1)}, f32[1024,2]{0,1:T(2,128)}, u32[]{:S(2)}) copy-start(f32[1024,2]{0,1:T(2,128)} %param.4) | copy-start | bytes 24580
  77.3 8.7 %copy-start.1 = (f32[1024]{0:T(1024)S(1)}, f32[1024]{0:T(1024)}, u32[]{:S(2)}) copy-start(f32[1024]{0:T(1024)} %param.5) | copy-start | bytes 12292
  77.3 326.0 %all-to-all-start = ((bf16[4,2,1600,1024]{3,2,1,0:T(8,128)(2,1)}), bf16[4,2,1600,1024]{3,2,1,0:T(8,128)(2,1)}, u32[]{:S(2)}, u32[]{:S(2)}) async-start(bf16[4,2,1600,1024]{3,2,1,0:T(8,128)(2,1)} %pad_maximum_fusion), calls=%async_computation | async-start | bytes 52428800 | tf_op jit(solution)/shard_map/all_to_all | solution.py:9

commit v2 on v0

--- a/solution.py
+++ b/solution.py
@@ -5,6 +5,21 @@
 
 
 def per_device(train_down, router_weight, router_gain):
+
+    def _render_leaves(mat, array_axis):
+        device_axis = "expert"
+        fields = []
+        num = lax.psum(1, device_axis)
+        for p in range(mat.ndim):
+            fields.append(num if p == array_axis else 1)
+        return lax.all_to_all(
+            jnp.tile(mat, fields),
+            device_axis,
+            split_axis=array_axis,
+            concat_axis=array_axis,
+            tiled=True,
+        )
+
     scale_down = lax.pmax(jnp.max(jnp.abs(train_down), axis=2), "shard")
     narrow_down = (train_down / jnp.expand_dims(scale_down, 2)).astype(jnp.bfloat16)
     ready_down = lax.all_to_all(narrow_down, "shard", split_axis=1, concat_axis=2, tiled=True)
@@ -13,7 +28,7 @@
     )
     part_router = (router_weight * router_gain[:, None]).astype(jnp.bfloat16)
     row_router = lax.all_gather(part_router, "shard", axis=0, tiled=True)
-    serve_router = lax.all_gather(row_router, "expert", axis=1, tiled=True)
+    serve_router = _render_leaves(row_router, 1)
     return (ready_down, scale_down, serve_router)
 
 

time: 508 us -> 487 us (0.959)
  blocking collectives: 329 us -> 18.1 us
  waiting for transfers between devices: 0.01 us -> 283 us
  starting transfers between devices: 8.59 us -> 14.8 us
    all_to_all x1, waiting for transfers between devices: 0.01 us -> 283 us  [per_device(): lax.all_to_all(narrow_down, 'shard', split_axis=1, concat_axis=2, tiled=T...]
    all_gather x1, blocking collectives: 285 us -> 6.25 us  [per_device(): row_router = lax.all_gather(part_router, 'shard', axis=0, tiled=True)]
    all_gather x1 -> x0, blocking collectives: 30.8 us -> none  [per_device(): serve_router = lax.all_gather(row_router, 'expert', axis=1, tiled=True)]
    all_to_all x0 -> x1, starting transfers between devices: none -> 6.22 us  [_render_leaves(): lax.all_to_all(jnp.tile(mat, fields), device_axis, split_axis=array_axis,...]
  transfers between devices with their start and end apart: 1 -> 2, of which waited for: 0 -> 1; matrix products, arithmetic and copies ran while one was open for 0% -> 19% of each run, Pallas kernels for 0% -> 0%
where the time goes in v2:
time: 487 us; the launch traced here: 485 us
  waiting for transfers between devices  283 us (58%)
  local copies, waits for them, and re-layouts  125 us (26%)
  other arithmetic  43.9 us (9%)
  blocking collectives  18.1 us (4%)
  starting transfers between devices  14.8 us (3%)
    all_to_all x1, waiting for transfers between devices, per_device(): lax.all_to_all(narrow_down, 'shard', split_axis=1, concat_axis=2, tiled=T...  283 us
    all_to_all x2, local copies, waits for them, and re-layouts, per_device(): lax.all_to_all(narrow_down, 'shard', split_axis=1, concat_axis=2, tiled=T...  75.8 us
    convert_element_type x1, local copies, waits for them, and re-layouts, per_device(): (train_down / jnp.expand_dims(scale_down, 2)).astype(jnp.bfloat16)  47.3 us
    convert_element_type x1, other arithmetic, per_device(): (train_down / jnp.expand_dims(scale_down, 2)).astype(jnp.bfloat16)  26.1 us
    reduce_max x1, other arithmetic, per_device(): scale_down = lax.pmax(jnp.max(jnp.abs(train_down), axis=2), 'shard')  17 us
    pmax x1, blocking collectives, per_device(): scale_down = lax.pmax(jnp.max(jnp.abs(train_down), axis=2), 'shard')  11.8 us
  transfers between devices with their start and end apart: 2, of which 1 were waited for; matrix products, arithmetic and copies ran while one was open for 19% of the time, Pallas kernels for 0%

profile of v2, /device:TPU:0, one launch (start us, length us, event | category | flops | bytes accessed | tf_op | source)
XLA Modules:
  0.0 485.4 jit_solution(18222184156977529834)
XLA Ops:
  0.6 0.7 multiply_convert_fusion
  1.3 6.3 %all_gather.3 = bf16[4096,2]{0,1:T(2,128)(2,1)S(1)} all-gather(bf16[1024,2]{0,1:T(2,128)(2,1)S(1)} %multiply_convert_fusion), channel_id=1, replica_groups=mesh['expert'=8,'shard'=4] {'shard'}, dimensions={0}, use_global_device_ids=true | all-gather | bytes 20480 | tf_op jit(solution)/shard_map/all_gather | solution.py:30
  7.6 0.7 tile.2
  8.3 6.2 %all-to-all-start.1 = ((bf16[4096,8,2]{0,2,1:T(2,128)(2,1)}), bf16[4096,8,2]{0,2,1:T(2,128)(2,1)S(1)}, u32[]{:S(2)}, u32[]{:S(2)}) async-start(bf16[4096,8,2]{0,2,1:T(2,128)(2,1)} %tile.2), calls=%async_computation.1 | async-start | bytes 262144 | tf_op jit(solution)/shard_map/all_to_all | solution.py:15
  14.5 17.0 %abs_reduce_fusion = f32[2,6400]{1,0:T(2,128)S(1)} fusion(f32[2,6400,1024]{2,1,0:T(8,128)} %param.3), kind=kLoop, calls=%fused_computation.1 | loop fusion | flops 26201600 | bytes 52480000 | tf_op jit(solution)/shard_map/reduce_max | solution.py:23
  31.6 11.8 %pmax.7 = f32[2,6400]{1,0:T(2,128)S(1)} all-reduce(f32[2,6400]{1,0:T(2,128)S(1)} %abs_reduce_fusion), channel_id=1, replica_groups=mesh['expert'=8,'shard'=4] {'shard'}, use_global_device_ids=true, to_apply=%region_1.0 | all-reduce | flops 12800 | bytes 102400 | tf_op jit(solution)/shard_map/pmax | solution.py:23
  43.4 26.1 %divide_convert_fusion = bf16[2,6400,1024]{2,1,0:T(8,128)(2,1)} fusion(f32[2,6400,1024]{2,1,0:T(8,128)} %param.3, f32[2,6400]{1,0:T(2,128)S(1)} %pmax.7), kind=kLoop, calls=%fused_computation | loop fusion | flops 26214400 | bytes 78694400 | tf_op jit(solution)/shard_map/convert_element_type | solution.py:24
  69.5 47.3 %copy.10 = bf16[2,6400,1024]{2,0,1:T(2,128)(2,1)} copy(bf16[2,6400,1024]{2,1,0:T(8,128)(2,1)} %divide_convert_fusion) | data formatting | bytes 52428800 | tf_op jit(solution)/shard_map/convert_element_type | solution.py:24
  116.9 0.0 all-to-all-done.1
  116.9 8.6 %all-to-all-start = ((bf16[2,6400,1024]{2,0,1:T(2,128)(2,1)}), bf16[2,6400,1024]{2,0,1:T(2,128)(2,1)}, u32[]{:S(2)}, u32[]{:S(2)}) async-start(bf16[2,6400,1024]{2,0,1:T(2,128)(2,1)} %copy.10), calls=%async_computation | async-start | bytes 52428800 | tf_op jit(solution)/shard_map/all_to_all | solution.py:25
  125.5 0.7 constant_dynamic-slice_fusion
  126.2 0.7 all_to_all.24
  126.9 282.7 %all-to-all-done = bf16[2,6400,1024]{2,0,1:T(2,128)(2,1)} async-done(((bf16[2,6400,1024]{2,0,1:T(2,128)(2,1)}), bf16[2,6400,1024]{2,0,1:T(2,128)(2,1)}, u32[]{:S(2)}, u32[]{:S(2)}) %all-to-all-start) | async-done | bytes 26214432 | tf_op jit(solution)/shard_map/all_to_all | solution.py:25
  409.6 33.3 %copy.11 = bf16[2,1600,4,1024]{3,2,1,0:T(4,128)(2,1)} copy(bf16[2,1600,4,1024]{3,0,1,2:T(2,128)(2,1)} %bitcast.1) | data formatting | bytes 52428800 | tf_op jit(solution)/shard_map/all_to_all | solution.py:25
  443.0 42.5 %all_to_all.22 = bf16[2,1600,4096]{2,1,0:T(8,128)(2,1)} reshape(bf16[2,1600,4,1024]{3,2,1,0:T(4,128)(2,1)} %copy.11) | data formatting | bytes 52428800 | tf_op jit(solution)/shard_map/all_to_all | solution.py:25
Async XLA Ops:
  8.3 108.5 %all-to-all-start.1 = ((bf16[4096,8,2]{0,2,1:T(2,128)(2,1)}), bf16[4096,8,2]{0,2,1:T(2,128)(2,1)S(1)}, u32[]{:S(2)}, u32[]{:S(2)}) async-start(bf16[4096,8,2]{0,2,1:T(2,128)(2,1)} %tile.2), calls=%async_computation.1 | async-start | bytes 262144 | tf_op jit(solution)/shard_map/all_to_all | solution.py:15
  116.9 292.8 %all-to-all-start = ((bf16[2,6400,1024]{2,0,1:T(2,128)(2,1)}), bf16[2,6400,1024]{2,0,1:T(2,128)(2,1)}, u32[]{:S(2)}, u32[]{:S(2)}) async-start(bf16[2,6400,1024]{2,0,1:T(2,128)(2,1)} %copy.10), calls=%async_computation | async-start | bytes 52428800 | tf_op jit(solution)/shard_map/all_to_all | solution.py:25
